TPU v7x, 512 devices: a whole 4x8x8 slice. The times are simulated.
512 devices in a mesh: tok: 64 (over y, x, core), ch: 8 (over z).
Axes of the slice: x: 4, y: 8, z: 8, core: 2. Of those that a mesh axis runs over, the one named last changes fastest.
Arguments:
- fields: float32 [16384, 1024], P('tok', 'ch'), may hold values from -20 to 20
- gain_one: float32 [1024], P('ch'), may hold values from 0.1 to 1.9
- tok_in_weight: float32 [3072, 16384], P('ch', 'tok'), may hold values from -0.046875 to 0.046875
- tok_in_bias: float32 [3072], P('ch'), may hold values from -3 to 3
- tok_out_weight: float32 [16384, 3072], P('tok', 'ch'), may hold values from -0.109375 to 0.109375
- gain_two: float32 [1024], P('ch'), may hold values from 0.1 to 1.9
- ch_in_weight: float32 [1024, 6144], P('tok', 'ch'), may hold values from -0.1875 to 0.1875
- ch_in_bias: float32 [6144], P('ch'), may hold values from -3 to 3
- ch_out_weight: float32 [6144, 1024], P('ch', 'tok'), may hold values from -0.078125 to 0.078125
Outputs:
- block_out: float32 [16384, 1024], P('tok', 'ch')
All inputs are finite; a program needn't handle non-finite values.
Results may differ from a plain program's by a relative error of at most 0.000086.
Values sent between devices are 32-bit elements; how exact they have to be, the bound alone decides.
A program may use at most 64 MiB of HBM per device.

v0:
```python
import jax
import jax.numpy as jnp
from jax import lax
from jax.sharding import PartitionSpec as P

epsilon = 1e-05
highest = lax.Precision.HIGHEST


def matmul(left, right):
    return jnp.dot(left, right, precision=highest, preferred_element_type=jnp.float32)


def shards(
    fields,
    gain_one,
    tok_in_weight,
    tok_in_bias,
    tok_out_weight,
    gain_two,
    ch_in_weight,
    ch_in_bias,
    ch_out_weight,
):
    tok_rows, ch_width = fields.shape
    channels = ch_width * lax.axis_size("ch")
    row_total = lax.psum(jnp.sum(fields, axis=1, keepdims=True), "ch")
    centred = fields - row_total / channels
    row_spread = lax.psum(jnp.sum(centred * centred, axis=1, keepdims=True), "ch")
    normed_part = centred * lax.rsqrt(row_spread / channels + epsilon) * gain_one
    normed = lax.all_gather(normed_part, "ch", axis=1, tiled=True)
    columns = normed
    summed_cols = lax.psum_scatter(
        lax.dot_general(
            columns,
            tok_in_weight,
            (((0,), (1,)), ((), ())),
            precision=highest,
            preferred_element_type=jnp.float32,
        ),
        "tok",
        scatter_dimension=0,
        tiled=True,
    )
    activated = jax.nn.gelu(summed_cols + tok_in_bias[None, :], approximate=False)
    partial_value = lax.dot_general(
        tok_out_weight,
        lax.all_gather(activated, "tok", axis=0, tiled=True),
        (((1,), (1,)), ((), ())),
        precision=highest,
        preferred_element_type=jnp.float32,
    )
    mixed_sum = lax.psum_scatter(partial_value, "ch", scatter_dimension=1, tiled=True)
    kept_rows = fields + mixed_sum
    row_total_two = lax.psum(jnp.sum(kept_rows, axis=1, keepdims=True), "ch")
    centred_two = kept_rows - row_total_two / channels
    row_spread_two = lax.psum(jnp.sum(centred_two * centred_two, axis=1, keepdims=True), "ch")
    normed_part_two = centred_two * lax.rsqrt(row_spread_two / channels + epsilon) * gain_two
    normed_two = lax.all_gather(normed_part_two, "ch", axis=1, tiled=True)
    columns = normed_two
    hidden_sum = matmul(columns, lax.all_gather(ch_in_weight, "tok", axis=0, tiled=True))
    activated_two = jax.nn.gelu(hidden_sum + ch_in_bias[None, :], approximate=False)
    channel_terms = matmul(activated_two, lax.all_gather(ch_out_weight, "tok", axis=1, tiled=True))
    return kept_rows + lax.psum_scatter(channel_terms, "ch", scatter_dimension=1, tiled=True)


def solution(mesh):
    in_specs = (
        P("tok", "ch"),
        P("ch"),
        P("ch", "tok"),
        P("ch"),
        P("tok", "ch"),
        P("ch"),
        P("tok", "ch"),
        P("ch"),
        P("ch", "tok"),
    )
    out_specs = P("tok", "ch")
    return jax.shard_map(shards, mesh=mesh, in_specs=in_specs, out_specs=out_specs, check_vma=False)
```

profile of v0, /device:TPU:2, one launch (start us, length us, event | category | flops | bytes accessed | tf_op | source)
XLA Modules:
  0.0 690.1 jit_solution(6796700619415421560)
XLA Ops:
  6.5 0.0 copy-start
  6.5 0.0 all-gather.6.cloned.1.call-start
  6.5 1.1 reduce_sum.36
  7.6 23.2 %psum.28 = f32[256,1]{0,1:T(1,128)S(1)} all-reduce(f32[256,1]{0,1:T(1,128)S(1)} %bitcast.25), channel_id=1, replica_groups=mesh['tok'=64,'ch'=8] {'ch'}, use_global_device_ids=true, to_apply=%region_1.0 | all-reduce | flops 256 | bytes 2048 | tf_op jit(solution)/shard_map/psum | solution.py:27
  30.8 1.1 multiply_reduce_fusion.1
  31.9 14.2 %psum.29 = f32[256,1]{0,1:T(1,128)S(1)} all-reduce(f32[256,1]{0,1:T(1,128)S(1)} %bitcast.26), channel_id=1, replica_groups=mesh['tok'=64,'ch'=8] {'ch'}, use_global_device_ids=true, to_apply=%region_3.0 | all-reduce | flops 256 | bytes 2048 | tf_op jit(solution)/shard_map/psum | solution.py:29
  46.1 1.7 multiply_multiply_fusion.6
  47.8 0.0 all-gather.6.cloned.1.call-update
  47.8 0.0 all-reduce.3.cloned.1.call-start
  47.9 40.3 %all-gather.6.cloned.1.call-done = f32[256,1024]{1,0:T(8,128)} async-done(((f32[256,128]{1,0:T(8,128)}), f32[256,1024]{1,0:T(8,128)}) %all-gather.6.cloned.1.call-update) | async-done | bytes 1048592 | tf_op jit(solution)/shard_map/all_gather | solution.py:31
  88.2 0.0 copy-done
  88.2 5.8 fusion.129
  94.0 0.0 all-reduce.3.cloned.1.call-update
  94.0 0.0 all-gather.8.cloned.1.call-start
  94.1 1.3 dynamic-slice
  96.0 197.0 %all-reduce.3.cloned.1.call-done = f32[1024,384]{1,0:T(8,128)} async-done(((f32[1024,384]{1,0:T(8,128)}), f32[1024,384]{1,0:T(8,128)}) %all-reduce.3.cloned.1.call-update) | async-done | bytes 1572880
  293.0 0.0 copy-done.4
  293.0 1.4 fusion.90
  294.4 0.0 all-gather.8.cloned.1.call-update
  294.4 0.0 reduce-scatter.3.cloned.1.call-start
  294.5 82.7 %all-gather.8.cloned.1.call-done = f32[1024,384]{1,0:T(8,128)} async-done(((f32[16,384]{1,0:T(8,128)}), f32[1024,384]{1,0:T(8,128)}) %all-gather.8.cloned.1.call-update) | async-done | bytes 1572880 | tf_op jit(solution)/shard_map/all_gather | solution.py:48
  377.1 0.0 copy-done.2
  377.2 4.2 convolution_bitcast_fusion
  381.3 0.0 reduce-scatter.3.cloned.1.call-update
  381.4 0.0 all-gather.12.cloned.1.call-start
  381.4 0.5 all-gather.12.cloned.1.call-update
  382.0 0.0 all-gather.10.cloned.1.call-start
  382.0 0.0 copy-done.1
  382.0 0.1 copy.16
  382.1 40.9 %reduce-scatter.3.cloned.1.call-done = f32[256,128]{0,1:T(8,128)} async-done(((f32[256,1024]{0,1:T(8,128)}), f32[256,128]{0,1:T(8,128)}) %reduce-scatter.3.cloned.1.call-update) | async-done | bytes 131088 | tf_op jit(solution)/shard_map/reduce_scatter | solution.py:53
  423.0 0.9 fusion.128
  424.0 15.4 %psum.30 = f32[256,1]{0,1:T(1,128)S(1)} all-reduce(f32[256,1]{0,1:T(1,128)S(1)} %bitcast.22), channel_id=1, replica_groups=mesh['tok'=64,'ch'=8] {'ch'}, use_global_device_ids=true, to_apply=%region_7.0 | all-reduce | flops 256 | bytes 2048 | tf_op jit(solution)/shard_map/psum | solution.py:55
  439.4 14.9 %psum.31 = f32[256,1]{0,1:T(1,128)S(1)} all-reduce(f32[256,1]{0,1:T(1,128)S(1)} %bitcast.27), channel_id=1, replica_groups=mesh['tok'=64,'ch'=8] {'ch'}, use_global_device_ids=true, to_apply=%region_9.0 | all-reduce | flops 256 | bytes 2048 | tf_op jit(solution)/shard_map/psum | solution.py:57
  454.3 0.0 copy-done.5
  454.3 0.7 multiply_multiply_fusion.5
  455.1 0.0 all-gather.10.cloned.1.call-update
  455.1 0.0 all-gather.14.cloned.1.call-start
  455.2 0.7 all-gather.14.cloned.1.call-update
  455.9 0.2 reduce-scatter.5.cloned.1.call-start
  456.1 50.2 %all-gather.12.cloned.1.call-done = f32[1024,768]{1,0:T(8,128)} async-done(((f32[16,768]{1,0:T(8,128)}), f32[1024,768]{1,0:T(8,128)}) %all-gather.12.cloned.1.call-update) | async-done | bytes 3145744 | tf_op jit(solution)/shard_map/all_gather | solution.py:61
  506.3 42.9 %all-gather.10.cloned.1.call-done = f32[256,1024]{0,1:T(8,128)} async-done(((f32[256,128]{0,1:T(8,128)}), f32[256,1024]{0,1:T(8,128)}) %all-gather.10.cloned.1.call-update) | async-done | bytes 1048592 | tf_op jit(solution)/shard_map/all_gather | solution.py:59
  549.2 5.0 convolution_add_fusion
  554.2 78.4 %all-gather.14.cloned.1.call-done = f32[768,1024]{0,1:T(8,128)} async-done(((f32[768,16]{0,1:T(8,128)}), f32[768,1024]{0,1:T(8,128)}) %all-gather.14.cloned.1.call-update) | async-done | bytes 3145744 | tf_op jit(solution)/shard_map/all_gather | solution.py:63
  632.7 7.3 %fusion.2 = f32[256,1024]{0,1:T(8,128)} fusion(f32[768,1024]{0,1:T(8,128)} %all-gather.14.cloned.1.call-done, f32[256,768]{1,0:T(8,128)S(1)} %convolution_add_fusion), kind=kOutput, calls=%fused_computation.5 | convolution fusion | flops 2428502016 | bytes 4980736 | tf_op jit(solution)/shard_map/dot_general | solution.py:11
  640.0 0.0 reduce-scatter.5.cloned.1.call-update
  640.0 41.6 %reduce-scatter.5.cloned.1.call-done = f32[256,128]{0,1:T(8,128)} async-done(((f32[256,1024]{0,1:T(8,128)}), f32[256,128]{0,1:T(8,128)}) %reduce-scatter.5.cloned.1.call-update) | async-done | bytes 131088 | tf_op jit(solution)/shard_map/reduce_scatter | solution.py:64
  681.6 0.9 add.49
  682.5 0.8 copy.18
  (11 shorter events, 0.1 us)
Async XLA Ops:
  6.5 81.7 %copy-start = (f32[384,256]{1,0:T(8,128)S(1)}, f32[384,256]{1,0:T(8,128)}, u32[]{:S(2)}) copy-start(f32[384,256]{1,0:T(8,128)} %param.11) | copy-start | bytes 1179652
  6.5 286.4 %copy-start.4 = (f32[384]{0:T(512)S(1)}, f32[384]{0:T(512)}, u32[]{:S(2)}) copy-start(f32[384]{0:T(512)} %param.12) | copy-start | bytes 4612
  6.5 370.6 %copy-start.2 = (f32[256,384]{1,0:T(8,128)S(1)}, f32[256,384]{1,0:T(8,128)}, u32[]{:S(2)}) copy-start(f32[256,384]{1,0:T(8,128)} %param.13) | copy-start | bytes 1179652
  6.5 81.6 %all-gather.6.cloned.1.call-start = ((), (), s32[]{:S(2)}) async-start(), calls=%async_computation.2 | async-start | bytes 1179648 | tf_op jit(solution)/shard_map/all_gather | solution.py:31
  47.8 245.2 %all-reduce.3.cloned.1.call-start = ((), (), s32[]{:S(2)}) async-start(), calls=%async_computation.9 | async-start | bytes 3145728
  94.0 288.0 %copy-start.1 = (f32[256,128]{1,0:T(8,128)S(1)}, f32[256,128]{1,0:T(8,128)}, u32[]{:S(2)}) copy-start(f32[256,128]{1,0:T(8,128)} %param.9) | copy-start | bytes 393220
  94.0 360.3 %copy-start.5 = (f32[128]{0:T(128)S(1)}, f32[128]{0:T(128)}, u32[]{:S(2)}) copy-start(f32[128]{0:T(128)} %param.14) | copy-start | bytes 1540
  94.0 455.2 %copy-start.3 = (f32[768]{0:T(1024)S(1)}, f32[768]{0:T(1024)}, u32[]{:S(2)}) copy-start(f32[768]{0:T(1024)} %param.16) | copy-start | bytes 9220
  94.0 283.1 %all-gather.8.cloned.1.call-start = ((), (), s32[]{:S(2)}) async-start(), calls=%async_computation.3 | async-start | bytes 1597440 | tf_op jit(solution)/shard_map/all_gather | solution.py:48
  294.4 128.6 %reduce-scatter.3.cloned.1.call-start = ((), (), s32[]{:S(2)}) async-start(), calls=%async_computation.4 | async-start | bytes 1179648 | tf_op jit(solution)/shard_map/reduce_scatter | solution.py:53
  381.4 125.0 %all-gather.12.cloned.1.call-start = ((), (), s32[]{:S(2)}) async-start(), calls=%async_computation.6 | async-start | bytes 3194880 | tf_op jit(solution)/shard_map/all_gather | solution.py:61
  382.0 167.3 %all-gather.10.cloned.1.call-start = ((), (), s32[]{:S(2)}) async-start(), calls=%async_computation.5 | async-start | bytes 1179648 | tf_op jit(solution)/shard_map/all_gather | solution.py:59
  455.1 177.6 %all-gather.14.cloned.1.call-start = ((), (), s32[]{:S(2)}) async-start(), calls=%async_computation.7 | async-start | bytes 3194880 | tf_op jit(solution)/shard_map/all_gather | solution.py:63
  455.9 225.7 %reduce-scatter.5.cloned.1.call-start = ((), (), s32[]{:S(2)}) async-start(), calls=%async_computation.8 | async-start | bytes 1179648 | tf_op jit(solution)/shard_map/reduce_scatter | solution.py:64
Sparse Core Ops, SparseCore 0:
  47.9 40.2 all-gather.5
  94.1 198.7 all-reduce.2
  296.3 80.7 all-gather.7
  381.5 41.4 reduce-scatter.2
  426.2 80.0 all-gather.11
  508.3 40.9 all-gather.9
  552.6 80.0 all-gather.13
  640.1 41.4 reduce-scatter.4
where the time goes:
time: 691 us; the launch traced here: 690 us
  waiting for transfers between devices  575 us (83%)
  blocking collectives  67.7 us (10%)
  matrix products  22.3 us (3%)
  between operations  14.2 us (2%)
  other arithmetic  7.95 us (1%)
    unnamed x9, waiting for transfers between devices  198 us
    all_gather x1, waiting for transfers between devices, shards(): lax.all_gather(activated, 'tok', axis=0, tiled=True)  82.7 us
    all_gather x1, waiting for transfers between devices, shards(): lax.all_gather(ch_out_weight, 'tok', axis=1, tiled=True)  78.4 us
    all_gather x1, waiting for transfers between devices, shards(): lax.all_gather(ch_in_weight, 'tok', axis=0, tiled=True)  50.2 us
    all_gather x1, waiting for transfers between devices, shards(): normed_two = lax.all_gather(normed_part_two, 'ch', axis=1, tiled=True)  42.9 us
    reduce_scatter x1, waiting for transfers between devices, shards(): lax.psum_scatter(channel_terms, 'ch', scatter_dimension=1, tiled=True)  41.6 us
    reduce_scatter x1, waiting for transfers between devices, shards(): lax.psum_scatter(partial_value, 'ch', scatter_dimension=1, tiled=True)  40.9 us
    all_gather x1, waiting for transfers between devices, shards(): normed = lax.all_gather(normed_part, 'ch', axis=1, tiled=True)  40.3 us
  transfers between devices with their start and end apart: 8, of which 8 were waited for; matrix products, arithmetic and copies ran while one was open for 1% of the time, Pallas kernels for 0%

commit v1 on v0

--- a/solution.py
+++ b/solution.py
@@ -45,7 +45,9 @@
     activated = jax.nn.gelu(summed_cols + tok_in_bias[None, :], approximate=False)
     partial_value = lax.dot_general(
         tok_out_weight,
-        lax.all_gather(activated, "tok", axis=0, tiled=True),
+        jnp.concatenate(
+            lax.all_to_all(jnp.stack([activated] * lax.axis_size("tok")), "tok", 0, 0), axis=0
+        ),
         (((1,), (1,)), ((), ())),
         precision=highest,
         preferred_element_type=jnp.float32,

time: 691 us -> 652 us (0.944)
  waiting for transfers between devices: 575 us -> 490 us
  blocking collectives: 67.7 us -> 116 us
    all_gather x1 -> x0, waiting for transfers between devices: 82.7 us -> none  [shards(): lax.all_gather(activated, 'tok', axis=0, tiled=True)]
    all_to_all x0 -> x1, blocking collectives: none -> 48.4 us  [shards(): lax.all_to_all(jnp.stack([activated] * lax.axis_size('tok')), 'tok', 0, 0)]
    unnamed x9 -> x8, waiting for transfers between devices: 198 us -> 198 us
  transfers between devices with their start and end apart: 8 -> 7, of which waited for: 8 -> 7; matrix products, arithmetic and copies ran while one was open for 1% -> 1% of each run, Pallas kernels for 0% -> 0%
where the time goes in v1:
time: 652 us; the launch traced here: 651 us
  waiting for transfers between devices  490 us (75%)
  blocking collectives  116 us (18%)
  matrix products  20.9 us (3%)
  between operations  14.2 us (2%)
  other arithmetic  7.32 us (1%)
    unnamed x8, waiting for transfers between devices  198 us
    all_gather x1, waiting for transfers between devices, shards(): lax.all_gather(ch_out_weight, 'tok', axis=1, tiled=True)  78.3 us
    all_gather x1, waiting for transfers between devices, shards(): lax.all_gather(ch_in_weight, 'tok', axis=0, tiled=True)  50.4 us
    all_to_all x1, blocking collectives, shards(): lax.all_to_all(jnp.stack([activated] * lax.axis_size('tok')), 'tok', 0, 0)  48.4 us
    all_gather x1, waiting for transfers between devices, shards(): normed_two = lax.all_gather(normed_part_two, 'ch', axis=1, tiled=True)  42.9 us
    reduce_scatter x1, waiting for transfers between devices, shards(): lax.psum_scatter(channel_terms, 'ch', scatter_dimension=1, tiled=True)  41.7 us
    all_gather x1, waiting for transfers between devices, shards(): normed = lax.all_gather(normed_part, 'ch', axis=1, tiled=True)  40.3 us
    reduce_scatter x1, waiting for transfers between devices, shards(): lax.psum_scatter(partial_value, 'ch', scatter_dimension=1, tiled=True)  38.4 us
  transfers between devices with their start and end apart: 7, of which 7 were waited for; matrix products, arithmetic and copies ran while one was open for 1% of the time, Pallas kernels for 0%

profile of v1, /device:TPU:2, one launch (start us, length us, event | category | flops | bytes accessed | tf_op | source)
XLA Modules:
  0.0 651.3 jit_solution(15267602252553994532)
XLA Ops:
  6.5 0.0 copy-start
  6.5 0.0 all-gather.5.cloned.1.call-start
  6.5 1.1 reduce_sum.36
  7.6 23.2 %psum.28 = f32[256,1]{0,1:T(1,128)S(1)} all-reduce(f32[256,1]{0,1:T(1,128)S(1)} %bitcast.27), channel_id=1, replica_groups=mesh['tok'=64,'ch'=8] {'ch'}, use_global_device_ids=true, to_apply=%region_1.0 | all-reduce | flops 256 | bytes 2048 | tf_op jit(solution)/shard_map/psum | solution.py:27
  30.8 1.1 multiply_reduce_fusion.1
  31.9 14.2 %psum.29 = f32[256,1]{0,1:T(1,128)S(1)} all-reduce(f32[256,1]{0,1:T(1,128)S(1)} %bitcast.28), channel_id=1, replica_groups=mesh['tok'=64,'ch'=8] {'ch'}, use_global_device_ids=true, to_apply=%region_3.0 | all-reduce | flops 256 | bytes 2048 | tf_op jit(solution)/shard_map/psum | solution.py:29
  46.1 1.7 multiply_multiply_fusion.6
  47.8 0.0 all-gather.5.cloned.1.call-update
  47.8 0.0 copy-start.4
  47.8 0.0 all-reduce.3.cloned.1.call-start
  47.8 40.3 %all-gather.5.cloned.1.call-done = f32[256,1024]{1,0:T(8,128)} async-done(((f32[256,128]{1,0:T(8,128)}), f32[256,1024]{1,0:T(8,128)}) %all-gather.5.cloned.1.call-update) | async-done | bytes 1048592 | tf_op jit(solution)/shard_map/all_gather | solution.py:31
  88.2 0.0 copy-done
  88.2 5.8 fusion.129
  94.0 0.0 all-reduce.3.cloned.1.call-update
  94.0 0.0 reduce-scatter.3.cloned.1.call-start
  94.0 1.3 dynamic-slice
  96.0 197.0 %all-reduce.3.cloned.1.call-done = f32[1024,384]{1,0:T(8,128)} async-done(((f32[1024,384]{1,0:T(8,128)}), f32[1024,384]{1,0:T(8,128)}) %all-reduce.3.cloned.1.call-update) | async-done | bytes 1572880
  292.9 0.0 copy-done.4
  292.9 0.8 fusion.90
  293.7 0.1 stack.2
  293.9 0.0 copy-start.2
  293.9 48.4 %all_to_all.5 = f32[64,16,384]{2,1,0:T(8,128)S(1)} all-to-all(f32[64,16,384]{2,1,0:T(8,128)S(1)} %stack.2), channel_id=1, replica_groups=mesh['tok'=64,'ch'=8] {'tok'}, dimensions={0} | all-to-all | bytes 3145728 | tf_op jit(solution)/shard_map/all_to_all | solution.py:49
  342.3 0.0 copy-done.2
  342.3 2.8 convolution_bitcast_fusion
  345.1 0.0 reduce-scatter.3.cloned.1.call-update
  345.1 0.0 all-gather.9.cloned.1.call-start
  345.2 0.5 all-gather.9.cloned.1.call-update
  345.7 0.0 all-gather.7.cloned.1.call-start
  345.7 0.0 copy-done.1
  345.8 0.1 copy.16
  345.9 38.4 %reduce-scatter.3.cloned.1.call-done = f32[256,128]{0,1:T(8,128)} async-done(((f32[256,1024]{0,1:T(8,128)}), f32[256,128]{0,1:T(8,128)}) %reduce-scatter.3.cloned.1.call-update) | async-done | bytes 131088 | tf_op jit(solution)/shard_map/reduce_scatter | solution.py:55
  384.2 0.9 fusion.128
  385.2 15.4 %psum.30 = f32[256,1]{0,1:T(1,128)S(1)} all-reduce(f32[256,1]{0,1:T(1,128)S(1)} %bitcast.24), channel_id=1, replica_groups=mesh['tok'=64,'ch'=8] {'ch'}, use_global_device_ids=true, to_apply=%region_7.0 | all-reduce | flops 256 | bytes 2048 | tf_op jit(solution)/shard_map/psum | solution.py:57
  400.7 14.9 %psum.31 = f32[256,1]{0,1:T(1,128)S(1)} all-reduce(f32[256,1]{0,1:T(1,128)S(1)} %bitcast.29), channel_id=1, replica_groups=mesh['tok'=64,'ch'=8] {'ch'}, use_global_device_ids=true, to_apply=%region_9.0 | all-reduce | flops 256 | bytes 2048 | tf_op jit(solution)/shard_map/psum | solution.py:59
  415.5 0.7 multiply_multiply_fusion.5
  416.3 0.0 all-gather.7.cloned.1.call-update
  416.3 0.0 all-gather.11.cloned.1.call-start
  416.4 0.5 all-gather.11.cloned.1.call-update
  416.9 0.2 reduce-scatter.5.cloned.1.call-start
  417.1 50.4 %all-gather.9.cloned.1.call-done = f32[1024,768]{1,0:T(8,128)} async-done(((f32[16,768]{1,0:T(8,128)}), f32[1024,768]{1,0:T(8,128)}) %all-gather.9.cloned.1.call-update) | async-done | bytes 3145744 | tf_op jit(solution)/shard_map/all_gather | solution.py:63
  467.5 42.9 %all-gather.7.cloned.1.call-done = f32[256,1024]{0,1:T(8,128)} async-done(((f32[256,128]{0,1:T(8,128)}), f32[256,1024]{0,1:T(8,128)}) %all-gather.7.cloned.1.call-update) | async-done | bytes 1048592 | tf_op jit(solution)/shard_map/all_gather | solution.py:61
  510.4 5.0 convolution_add_fusion
  515.4 78.3 %all-gather.11.cloned.1.call-done = f32[768,1024]{0,1:T(8,128)} async-done(((f32[768,16]{0,1:T(8,128)}), f32[768,1024]{0,1:T(8,128)}) %all-gather.11.cloned.1.call-update) | async-done | bytes 3145744 | tf_op jit(solution)/shard_map/all_gather | solution.py:65
  593.7 7.3 %fusion.2 = f32[256,1024]{0,1:T(8,128)} fusion(f32[768,1024]{0,1:T(8,128)} %all-gather.11.cloned.1.call-done, f32[256,768]{1,0:T(8,128)S(1)} %convolution_add_fusion), kind=kOutput, calls=%fused_computation.5 | convolution fusion | flops 2428502016 | bytes 4980736 | tf_op jit(solution)/shard_map/dot_general | solution.py:11
  601.0 0.0 reduce-scatter.5.cloned.1.call-update
  601.0 41.7 %reduce-scatter.5.cloned.1.call-done = f32[256,128]{0,1:T(8,128)} async-done(((f32[256,1024]{0,1:T(8,128)}), f32[256,128]{0,1:T(8,128)}) %reduce-scatter.5.cloned.1.call-update) | async-done | bytes 131088 | tf_op jit(solution)/shard_map/reduce_scatter | solution.py:66
  642.8 0.9 add.49
  643.7 0.8 copy.18
  (10 shorter events, 0.1 us)
Async XLA Ops:
  6.5 81.6 %copy-start = (f32[384,256]{1,0:T(8,128)S(1)}, f32[384,256]{1,0:T(8,128)}, u32[]{:S(2)}) copy-start(f32[384,256]{1,0:T(8,128)} %param.11) | copy-start | bytes 1179652
  6.5 81.6 %all-gather.5.cloned.1.call-start = ((), (), s32[]{:S(2)}) async-start(), calls=%async_computation.3 | async-start | bytes 1179648 | tf_op jit(solution)/shard_map/all_gather | solution.py:31
  47.8 245.2 %copy-start.4 = (f32[384]{0:T(512)S(1)}, f32[384]{0:T(512)}, u32[]{:S(2)}) copy-start(f32[384]{0:T(512)} %param.12) | copy-start | bytes 4612
  47.8 245.1 %all-reduce.3.cloned.1.call-start = ((), (), s32[]{:S(2)}) async-start(), calls=%async_computation.9 | async-start | bytes 3145728
  94.0 290.2 %reduce-scatter.3.cloned.1.call-start = ((), (), s32[]{:S(2)}) async-start(), calls=%async_computation.4 | async-start | bytes 1179648 | tf_op jit(solution)/shard_map/reduce_scatter | solution.py:55
  293.9 48.4 %copy-start.2 = (f32[256,384]{1,0:T(8,128)S(1)}, f32[256,384]{1,0:T(8,128)}, u32[]{:S(2)}) copy-start(f32[256,384]{1,0:T(8,128)} %param.13) | copy-start | bytes 1179652
  342.3 3.4 copy-start.1
  345.1 70.5 %copy-start.5 = (f32[128]{0:T(128)S(1)}, f32[128]{0:T(128)}, u32[]{:S(2)}) copy-start(f32[128]{0:T(128)} %param.14) | copy-start | bytes 1540
  345.1 165.3 %copy-start.3 = (f32[768]{0:T(1024)S(1)}, f32[768]{0:T(1024)}, u32[]{:S(2)}) copy-start(f32[768]{0:T(1024)} %param.16) | copy-start | bytes 9220
  345.1 122.4 %all-gather.9.cloned.1.call-start = ((), (), s32[]{:S(2)}) async-start(), calls=%async_computation.6 | async-start | bytes 3194880 | tf_op jit(solution)/shard_map/all_gather | solution.py:63
  345.7 164.7 %all-gather.7.cloned.1.call-start = ((), (), s32[]{:S(2)}) async-start(), calls=%async_computation.5 | async-start | bytes 1179648 | tf_op jit(solution)/shard_map/all_gather | solution.py:61
  416.3 177.4 %all-gather.11.cloned.1.call-start = ((), (), s32[]{:S(2)}) async-start(), calls=%async_computation.7 | async-start | bytes 3194880 | tf_op jit(solution)/shard_map/all_gather | solution.py:65
  416.9 225.9 %reduce-scatter.5.cloned.1.call-start = ((), (), s32[]{:S(2)}) async-start(), calls=%async_computation.8 | async-start | bytes 1179648 | tf_op jit(solution)/shard_map/reduce_scatter | solution.py:66
Sparse Core Ops, SparseCore 0:
  47.9 40.2 all-gather.4
  94.1 198.7 all-reduce.2
  345.2 38.9 reduce-scatter.2
  387.4 80.0 all-gather.8
  469.4 40.9 all-gather.6
  513.6 80.0 all-gather.10
  601.1 41.5 reduce-scatter.4
